TPU v7x, 32 devices: a whole 2x2x4 slice. The times are simulated.
32 devices in a mesh: grp: 4 (over x, core), clu: 8 (over z, y).
Axes of the slice: x: 2, y: 2, z: 4, core: 2. Of those that a mesh axis runs over, the one named last changes fastest.
Arguments:
- radiosity: float32 [128, 3, 128], P(('grp', 'clu')), may hold values from 0 to 3
- form_factors: float32 [4096, 128, 128], P(('grp', 'clu')), may hold values from 0.01 to 16
- source_device: int32 [4096, 1], P(('grp', 'clu')), may hold values from 0 to 31; in each aligned block of 128 rows (0 to 127, 128 to 255, ...) at most 8 rows name the same one
- source_slot: int32 [4096], P(('grp', 'clu')), may hold values from 0 to 3
- receiver_slot: int32 [4096], P(('grp', 'clu')), may hold values from 0 to 3
- emission: float32 [128, 3, 128], P(('grp', 'clu')), may hold values from 0.1 to 2
- reflectance: float32 [128, 3, 128], P(('grp', 'clu')), may hold values from 0.3 to 0.9
- patch_area: float32 [128, 128], P(('grp', 'clu')), may hold values from 0.5 to 2
- cluster_group: int32 [128], P(('grp', 'clu')), may hold values from 0 to 15, as said below
- group_coupling: float32 [16, 16], replicated, may hold values from 0 to 1
- ambient: float32 [3], replicated, may hold values from 0.2 to 1
Outputs:
- radiosity_new: float32 [128, 3, 128], P(('grp', 'clu'))
- group_radiosity: float32 [16, 3], replicated
Inputs may be any that keep to these rules, and one draw needn't show every extreme that they name: `source_device`: the rows of one device name each source device at most 8 times. `cluster_group`: each group node has exactly 8 clusters.
All inputs are finite; a program needn't handle non-finite values.
Results may differ from a plain program's by a relative error of at most 0.00005.
Values sent between devices are 32-bit elements; how exact they have to be, the bound alone decides.
No kernel may reach another device: no remote copies, remote signals or barrier semaphores. Data moves between devices by JAX's collectives and lax.ppermute only.
A program may use at most 64 MiB of HBM per device.

v0:
```python
import jax
import jax.numpy as jnp
from jax import lax
from jax.sharding import PartitionSpec as P


def cluster_sums(field, patch_area):
    return jnp.einsum("kci,ki->kc", field, patch_area, precision=lax.Precision.HIGHEST)


def on_device(
    radiosity,
    form_factors,
    source_device,
    source_slot,
    receiver_slot,
    emission,
    reflectance,
    patch_area,
    cluster_group,
    group_coupling,
    ambient,
):
    clusters_here = radiosity.shape[0]
    count = form_factors.shape[0]
    width = form_factors.shape[1]
    groups_all = group_coupling.shape[0]
    devices = lax.axis_size("grp") * lax.axis_size("clu")
    scale = 2.0 * clusters_here / (width * count)
    sources = source_device[:, 0]
    capacity = max(2, 2 * count // devices)
    order = jnp.arange(count, dtype=jnp.int32)
    earlier = (sources[None, :] == sources[:, None]) & (order[None, :] < order[:, None])
    ranking = jnp.sum(earlier.astype(jnp.int32), axis=1)
    position = sources * capacity + ranking
    wanted = jnp.zeros((devices * capacity,), jnp.int32).at[position].set(source_slot + 1)
    asked = lax.all_to_all(
        wanted.reshape(devices, capacity), ("grp", "clu"), split_axis=0, concat_axis=0, tiled=True
    ).reshape(devices * capacity)
    valid = (asked > 0).astype(jnp.float32)
    answer = jnp.take(radiosity, jnp.maximum(asked - 1, 0), axis=0) * valid[:, None, None]
    returned = lax.all_to_all(
        answer.reshape(devices, capacity, 3, width),
        ("grp", "clu"),
        split_axis=0,
        concat_axis=0,
        tiled=True,
    ).reshape(devices * capacity, 3, width)
    fetched = jnp.take(returned, position, axis=0)
    contribution = (
        jnp.einsum("lij,lcj->lci", form_factors, fetched, precision=lax.Precision.HIGHEST) * scale
    )
    receiver_table = (
        receiver_slot[:, None] == jnp.arange(clusters_here, dtype=jnp.int32)[None, :]
    ).astype(jnp.float32)
    irradiance = jnp.einsum(
        "lk,lci->kci", receiver_table, contribution, precision=lax.Precision.HIGHEST
    )
    group_table = (
        cluster_group[:, None] == jnp.arange(groups_all, dtype=jnp.int32)[None, :]
    ).astype(jnp.float32)
    local_sum = jnp.dot(
        group_table.T, cluster_sums(radiosity, patch_area), precision=lax.Precision.HIGHEST
    )
    local_area = jnp.dot(
        group_table.T, jnp.sum(patch_area, axis=1), precision=lax.Precision.HIGHEST
    )
    group_sum, group_area = lax.psum((local_sum, local_area), ("grp", "clu"))
    old_group = group_sum / group_area[:, None]
    old_root = jnp.sum(group_sum, axis=0) / jnp.sum(group_area)
    group_irradiance = jnp.dot(
        group_coupling / groups_all, old_group, precision=lax.Precision.HIGHEST
    )
    coarse = (
        jnp.dot(group_table, group_irradiance, precision=lax.Precision.HIGHEST)
        + (ambient * old_root)[None, :]
    )
    radiosity_new = emission + reflectance * (irradiance + coarse[:, :, None])
    new_local = jnp.dot(
        group_table.T, cluster_sums(radiosity_new, patch_area), precision=lax.Precision.HIGHEST
    )
    new_sum = lax.psum(new_local, ("grp", "clu"))
    return (radiosity_new, new_sum / group_area[:, None])


def solution(mesh):
    return jax.shard_map(
        on_device,
        mesh=mesh,
        in_specs=(
            P(("grp", "clu"), None, None),
            P(("grp", "clu"), None, None),
            P(("grp", "clu"), None),
            P(("grp", "clu")),
            P(("grp", "clu")),
            P(("grp", "clu"), None, None),
            P(("grp", "clu"), None, None),
            P(("grp", "clu"), None),
            P(("grp", "clu")),
            P(),
            P(),
        ),
        out_specs=(P(("grp", "clu"), None, None), P()),
        check_vma=False,
    )
```

profile of v0, /device:TPU:0, one launch (start us, length us, event | category | flops | bytes accessed | tf_op | source)
XLA Modules:
  0.0 133.1 jit_solution(4761366920443387148)
XLA Ops:
  0.6 0.0 copy-start
  0.6 0.9 convert_reduce_fusion
  1.6 0.7 and_bitcast_fusion
  2.2 0.7 broadcast_add_fusion
  2.9 1.0 scatter_custom_fusion
  3.9 0.7 all_to_all.9
  4.5 7.3 %all-to-all-start = ((s32[32,1,8]{2,1,0:T(1,128)}), s32[32,1,8]{2,1,0:T(1,128)S(1)}, u32[]{:S(2)}, u32[]{:S(2)}) async-start(s32[32,1,8]{2,1,0:T(1,128)} %bitcast.5), calls=%async_computation | async-start | bytes 32768 | tf_op jit(solution)/shard_map/all_to_all | solution.py:37
  11.9 0.0 copy-done
  11.9 0.1 reduce_sum.40
  12.0 0.8 fusion.12
  12.9 0.9 fusion.18
  13.7 0.8 convolution_bitcast_fusion
  14.5 40.4 %all-reduce = (f32[16,3]{0,1:T(4,128)S(1)}, f32[16]{0:T(128)S(1)}) all-reduce(f32[16,3]{0,1:T(4,128)S(1)} %fusion.18, f32[16]{0:T(128)S(1)} %convolution_bitcast_fusion), channel_id=1, replica_groups=mesh['grp'=4,'clu'=8] {'grp','clu'}, use_global_device_ids=true, to_apply=%region_2.3 | all-reduce | flops 64 | bytes 512 | tf_op jit(solution)/shard_map/psum | solution.py:68
  54.9 0.6 reduce_sum.42
  55.5 0.1 reduce_sum.41
  55.7 0.0 all-to-all-done
  55.7 0.1 copy.28
  55.7 0.1 copy.33
  55.8 0.1 copy.29
  55.9 0.1 copy.30
  56.0 0.1 reshape.76
  56.1 0.0 copy-start.1
  56.1 0.0 copy-start.2
  56.1 0.0 copy-start.4
  56.1 0.0 copy-start.5
  56.1 2.1 %gather_fusion = f32[256,3,128]{2,0,1:T(8,128)S(1)} fusion(f32[4,3,128]{2,0,1:T(4,128)} %param.11, s32[1024]{0:T(1024)S(1)} %pad_clamp_fusion.1), kind=kCustom, calls=%fused_computation | custom fusion | bytes 787456 | tf_op jit(solution)/shard_map/jit(_take)/gather | solution.py:41
  58.2 0.9 fusion.2
  59.1 4.5 %all-to-all-start.1 = ((f32[32,8,3,128]{3,1,2,0:T(8,128)}), f32[32,8,3,128]{3,1,2,0:T(8,128)S(1)}, u32[]{:S(2)}, u32[]{:S(2)}) async-start(f32[32,8,3,128]{3,1,2,0:T(8,128)} %fusion.2), calls=%async_computation.1 | async-start | bytes 786432 | tf_op jit(solution)/shard_map/all_to_all | solution.py:42
  63.6 1.3 divide_multiply_fusion
  64.9 0.8 fusion.8
  65.7 0.8 convolution_add_fusion.1
  66.6 10.4 %all-to-all-done.1 = f32[32,8,3,128]{3,1,2,0:T(8,128)S(1)} async-done(((f32[32,8,3,128]{3,1,2,0:T(8,128)}), f32[32,8,3,128]{3,1,2,0:T(8,128)S(1)}, u32[]{:S(2)}, u32[]{:S(2)}) %all-to-all-start.1) | async-done | bytes 393248 | tf_op jit(solution)/shard_map/all_to_all | solution.py:42
  77.0 0.1 copy.34
  77.2 0.8 gather_fusion.1
  77.9 15.5 %convolution_multiply_fusion = f32[128,3,128]{2,1,0:T(4,128)S(1)} fusion(f32[128,128,128]{2,1,0:T(8,128)} %param.12, f32[128,3,128]{2,1,0:T(4,128)S(1)} %gather_fusion.1, pred[128]{0:T(512)(128)(4,1)S(1)} %get-tuple-element.4), kind=kOutput, calls=%fused_computation.3 | convolution fusion | flops 75595776 | bytes 8781952 | tf_op jit(solution)/shard_map/lij,lcj->lci/dot_general | solution.py:51
  93.4 0.0 copy-done.1
  93.4 0.0 copy-done.2
  93.4 0.0 copy-done.4
  93.4 0.2 fusion.1
  93.6 0.0 copy-start.3
  93.6 0.2 fusion.10
  93.8 0.0 copy-done.5
  93.8 0.2 fusion.17
  94.0 38.5 %psum.23 = f32[16,3]{0,1:T(4,128)S(1)} all-reduce(f32[16,3]{0,1:T(4,128)S(1)} %fusion.17), channel_id=1, replica_groups=mesh['grp'=4,'clu'=8] {'grp','clu'}, use_global_device_ids=true, to_apply=%region_7.8 | all-reduce | flops 48 | bytes 384 | tf_op jit(solution)/shard_map/psum | solution.py:82
  132.5 0.6 broadcast_divide_fusion
  133.1 0.0 copy-done.3
  (4 shorter events, 0.0 us)
Async XLA Ops:
  0.6 11.3 %copy-start = (f32[4,128]{1,0:T(4,128)S(1)}, f32[4,128]{1,0:T(4,128)}, u32[]{:S(2)}) copy-start(f32[4,128]{1,0:T(4,128)} %param.18) | copy-start | bytes 6148
  4.5 51.1 %all-to-all-start = ((s32[32,1,8]{2,1,0:T(1,128)}), s32[32,1,8]{2,1,0:T(1,128)S(1)}, u32[]{:S(2)}, u32[]{:S(2)}) async-start(s32[32,1,8]{2,1,0:T(1,128)} %bitcast.5), calls=%async_computation | async-start | bytes 32768 | tf_op jit(solution)/shard_map/all_to_all | solution.py:37
  56.1 37.3 %copy-start.1 = (f32[4,3,128]{2,0,1:T(4,128)S(1)}, f32[4,3,128]{2,0,1:T(4,128)}, u32[]{:S(2)}) copy-start(f32[4,3,128]{2,0,1:T(4,128)} %param.16) | copy-start | bytes 18436
  56.1 37.3 %copy-start.2 = (f32[4,3,128]{2,0,1:T(4,128)S(1)}, f32[4,3,128]{2,0,1:T(4,128)}, u32[]{:S(2)}) copy-start(f32[4,3,128]{2,0,1:T(4,128)} %param.17) | copy-start | bytes 18436
  56.1 37.3 %copy-start.4 = (s32[128]{0:T(128)S(1)}, s32[128]{0:T(128)}, u32[]{:S(2)}) copy-start(s32[128]{0:T(128)} %param.15) | copy-start | bytes 1540
  56.1 37.6 %copy-start.5 = (s32[4]{0:T(128)S(1)}, s32[4]{0:T(128)}, u32[]{:S(2)}) copy-start(s32[4]{0:T(128)} %param.19) | copy-start | bytes 52
  59.1 17.9 %all-to-all-start.1 = ((f32[32,8,3,128]{3,1,2,0:T(8,128)}), f32[32,8,3,128]{3,1,2,0:T(8,128)S(1)}, u32[]{:S(2)}, u32[]{:S(2)}) async-start(f32[32,8,3,128]{3,1,2,0:T(8,128)} %fusion.2), calls=%async_computation.1 | async-start | bytes 786432 | tf_op jit(solution)/shard_map/all_to_all | solution.py:42
  93.6 39.5 %copy-start.3 = (f32[4,3,128]{2,0,1:T(4,128)}, f32[4,3,128]{2,0,1:T(4,128)S(1)}, u32[]{:S(2)}) copy-start(f32[4,3,128]{2,0,1:T(4,128)S(1)} %fusion.1) | copy-start | bytes 18436
where the time goes:
time: 134 us; the launch traced here: 133 us
  blocking collectives  79 us (59%)
  matrix products  20.2 us (15%)
  starting transfers between devices  11.8 us (9%)
  waiting for transfers between devices  10.4 us (8%)
  other arithmetic  5.86 us (4%)
  local copies, waits for them, and re-layouts  5.07 us (4%)
    psum x1, blocking collectives, on_device(): group_sum, group_area = lax.psum((local_sum, local_area), ('grp', 'clu'))  40.4 us
    psum x1, blocking collectives, on_device(): new_sum = lax.psum(new_local, ('grp', 'clu'))  38.5 us
    dot_general x1, matrix products, on_device(): jnp.einsum('lij,lcj->lci', form_factors, fetched, precision=lax.Precision...  15.5 us
    all_to_all x1, waiting for transfers between devices, on_device(): lax.all_to_all(answer.reshape(devices, capacity, 3, width), ('grp', 'clu'...  10.4 us
    all_to_all x1, starting transfers between devices, on_device(): lax.all_to_all(wanted.reshape(devices, capacity), ('grp', 'clu'), split_a...  7.33 us
    all_to_all x1, starting transfers between devices, on_device(): lax.all_to_all(answer.reshape(devices, capacity, 3, width), ('grp', 'clu'...  4.48 us
  transfers between devices with their start and end apart: 2, of which 1 were waited for; matrix products, arithmetic and copies ran while one was open for 5% of the time, Pallas kernels for 0%

commit v1 on v0

v1 whole, which is shorter than its diff:
```python
import functools

import jax
import jax.numpy as jnp
from jax import lax
from jax.experimental import pallas as pl
from jax.experimental.pallas import tpu as pltpu
from jax.sharding import PartitionSpec as P

LANES = 128
AXES = ("grp", "clu")
VMEM = pl.BlockSpec(memory_space=pltpu.VMEM)
SMEM = pl.BlockSpec(memory_space=pltpu.SMEM)


def rows_for(quantities, groups):
    return -(-quantities // (LANES // groups))


def place(values, cluster_group_ref, groups):
    per_row = LANES // groups
    lane = lax.broadcasted_iota(jnp.int32, (1, LANES), 1)
    rows = [jnp.zeros((1, LANES), jnp.float32) for _ in range(rows_for(len(values), groups))]
    for q, of_clusters in enumerate(values):
        for k, value in enumerate(of_clusters):
            spot = (q % per_row) * groups + cluster_group_ref[k]
            rows[q // per_row] += jnp.where(lane == spot, value, 0.0)
    return rows


def pack_kernel(devices, groups, radiosity_ref, area_ref, cluster_group_ref, out_ref):
    channels, clusters, _ = radiosity_ref.shape
    area = area_ref[...]
    sums = [
        jnp.sum(radiosity_ref[c] * area, axis=1, keepdims=True) for c in range(channels)
    ] + [jnp.sum(area, axis=1, keepdims=True)]
    values = [[s[k : k + 1] for k in range(clusters)] for s in sums]
    info = place(values, cluster_group_ref, groups)
    rows = [radiosity_ref[c, k : k + 1] for c in range(channels) for k in range(clusters)] + info
    block = len(rows)
    for d in range(devices):
        for r, row in enumerate(rows):
            out_ref[d * block + r] = row


def sweep_kernel(
    devices,
    groups,
    scale,
    source_device_ref,
    source_slot_ref,
    receiver_slot_ref,
    cluster_group_ref,
    ambient_ref,
    gathered_ref,
    factors_ref,
    emission_ref,
    reflectance_ref,
    area_ref,
    coupling_ref,
    radiosity_ref,
    share_ref,
    acc_ref,
):
    channels, clusters, width = emission_ref.shape
    count = factors_ref.shape[0]
    blocks = width // 8
    block_rows = gathered_ref.shape[0] // devices
    own_rows = channels * clusters
    per_row = LANES // groups

    acc_ref[...] = jnp.zeros_like(acc_ref)

    totals = []
    for r in range(own_rows, block_rows):
        total = gathered_ref[r]
        for d in range(1, devices):
            total = total + gathered_ref[d * block_rows + r]
        totals.append(total)
    lane = lax.broadcasted_iota(jnp.int32, (1, LANES), 1)
    inside = lane < groups
    parts = []
    for q in range(channels + 1):
        row, shift = totals[q // per_row], (q % per_row) * groups
        part = pltpu.roll(row, LANES - shift, 1) if shift else row
        parts.append(jnp.where(inside, part, 0.0))
    group_area = jnp.where(inside, parts[channels], 1.0)
    all_area = jnp.sum(parts[channels], axis=1, keepdims=True)
    coarse = []
    for c in range(channels):
        old_group = parts[c] / group_area
        root = ambient_ref[c] * (jnp.sum(parts[c], axis=1, keepdims=True) / all_area)
        coarse.append(
            [
                jnp.sum(
                    coupling_ref[pl.ds(cluster_group_ref[k], 1), :] * old_group[:, :groups],
                    axis=1,
                    keepdims=True,
                )
                / groups
                + root
                for k in range(clusters)
            ]
        )

    def link(l, _):
        first = source_device_ref[l] * block_rows + source_slot_ref[l]
        k = receiver_slot_ref[l]
        rows = [
            jnp.broadcast_to(gathered_ref[first + c * clusters], (8, width))
            for c in range(channels)
        ]
        for b in range(blocks):
            f = factors_ref[l, b * 8 : (b + 1) * 8, :]
            for c in range(channels):
                acc_ref[k, c, b] += f * rows[c]
        return 0

    lax.fori_loop(0, count, link, 0, unroll=4)

    patch = lax.broadcasted_iota(jnp.int32, (blocks, 8, width), 0) * 8 + lax.broadcasted_iota(
        jnp.int32, (blocks, 8, width), 1
    )
    diagonal = patch == lax.broadcasted_iota(jnp.int32, (blocks, 8, width), 2)
    sums = [[None] * clusters for _ in range(channels)]
    for k in range(clusters):
        for c in range(channels):
            column = jnp.sum(acc_ref[k, c], axis=2, keepdims=True)
            spread = jnp.sum(jnp.where(diagonal, column, 0.0), axis=0)
            irradiance = jnp.sum(spread, axis=0, keepdims=True) * scale
            new = emission_ref[c, k : k + 1] + reflectance_ref[c, k : k + 1] * (
                irradiance + coarse[c][k]
            )
            radiosity_ref[c, k : k + 1] = new
            sums[c][k] = jnp.sum(new * area_ref[k : k + 1], axis=1, keepdims=True)
    rows = place(sums, cluster_group_ref, groups)
    wide_area = group_area
    for q in range(1, per_row):
        wide_area = jnp.where(lane >= q * groups, pltpu.roll(group_area, q * groups, 1), wide_area)
    for r in range(len(rows)):
        row = rows[r] / wide_area
        for d in range(devices):
            share_ref[d * len(rows) + r] = row


def total_kernel(devices, groups, channels, share_ref, out_ref):
    per_row = LANES // groups
    count = share_ref.shape[0] // devices
    rows = []
    for r in range(count):
        total = share_ref[r]
        for d in range(1, devices):
            total = total + share_ref[d * count + r]
        rows.append(total)
    for c in range(channels):
        row, shift = rows[c // per_row], (c % per_row) * groups
        part = pltpu.roll(row, LANES - shift, 1) if shift else row
        out_ref[c : c + 1, :] = part[:, :groups]


def on_device(
    radiosity,
    form_factors,
    source_device,
    source_slot,
    receiver_slot,
    emission,
    reflectance,
    patch_area,
    cluster_group,
    group_coupling,
    ambient,
):
    clusters, channels, width = radiosity.shape
    count = form_factors.shape[0]
    groups = group_coupling.shape[0]
    devices = lax.axis_size("grp") * lax.axis_size("clu")
    scale = 2.0 * clusters / (width * count)
    block = channels * clusters + rows_for(channels + 1, groups)
    by_channel = functools.partial(jnp.transpose, axes=(1, 0, 2))

    packed = pl.pallas_call(
        functools.partial(pack_kernel, devices, groups),
        out_shape=jax.ShapeDtypeStruct((devices * block, 1, LANES), jnp.float32),
        in_specs=[VMEM, VMEM, SMEM],
        out_specs=VMEM,
        name="pack",
    )(by_channel(radiosity), patch_area, cluster_group)
    gathered = lax.all_to_all(packed, AXES, split_axis=0, concat_axis=0, tiled=True)

    share_rows = rows_for(channels, groups)
    new, share = pl.pallas_call(
        functools.partial(sweep_kernel, devices, groups, scale),
        out_shape=(
            jax.ShapeDtypeStruct((channels, clusters, width), jnp.float32),
            jax.ShapeDtypeStruct((devices * share_rows, 1, LANES), jnp.float32),
        ),
        in_specs=[SMEM] * 5 + [VMEM] * 6,
        out_specs=(VMEM, VMEM),
        scratch_shapes=[pltpu.VMEM((clusters, channels, width // 8, 8, width), jnp.float32)],
        name="sweep",
    )(
        source_device[:, 0],
        source_slot,
        receiver_slot,
        cluster_group,
        ambient,
        gathered,
        form_factors,
        by_channel(emission),
        by_channel(reflectance),
        patch_area,
        group_coupling,
    )
    shares = lax.all_to_all(share, AXES, split_axis=0, concat_axis=0, tiled=True)
    total = pl.pallas_call(
        functools.partial(total_kernel, devices, groups, channels),
        out_shape=jax.ShapeDtypeStruct((channels, groups), jnp.float32),
        in_specs=[VMEM],
        out_specs=VMEM,
        name="total",
    )(shares)
    return by_channel(new), total.T


def solution(mesh):
    split = AXES
    return jax.shard_map(
        on_device,
        mesh=mesh,
        in_specs=(
            P(split, None, None),
            P(split, None, None),
            P(split, None),
            P(split),
            P(split),
            P(split, None, None),
            P(split, None, None),
            P(split, None),
            P(split),
            P(),
            P(),
        ),
        out_specs=(P(split, None, None), P()),
        check_vma=False,
    )
```

time: 134 us -> 37.8 us (0.28)
  blocking collectives: 79 us -> 26.6 us
  matrix products: 20.2 us -> 0 us
  starting transfers between devices: 11.8 us -> 0 us
  waiting for transfers between devices: 10.4 us -> 0 us
  Pallas kernels: 0 us -> 10.2 us
  other arithmetic: 5.86 us -> 0 us
  local copies, waits for them, and re-layouts: 5.07 us -> 0 us
    psum x2 -> x0, blocking collectives: 79 us -> none  [the longest x1 40.4 us: on_device(): group_sum, group_area = lax.psum((local_sum, local_area), ('grp', 'clu'))]
    all_to_all x0 -> x2, blocking collectives: none -> 26.6 us  [the longest x1 16.2 us: on_device(): lax.all_to_all(packed, AXES, split_axis=0, concat_axis=0, tiled=True)]
    dot_general x9 -> x0, matrix products: 20.2 us -> none  [the longest x1 15.5 us: on_device(): jnp.einsum('lij,lcj->lci', form_factors, fetched, precision=lax.Precision...]
    all_to_all x2 -> x0, starting transfers between devices: 11.8 us -> none  [the longest x1 7.33 us: on_device(): lax.all_to_all(wanted.reshape(devices, capacity), ('grp', 'clu'), split_a...]
    all_to_all x2 -> x0, waiting for transfers between devices: 10.4 us -> none  [the longest x1 10.4 us: on_device(): lax.all_to_all(answer.reshape(devices, capacity, 3, width), ('grp', 'clu'...]
    pallas_call x0 -> x3, Pallas kernels: none -> 10.2 us  [the longest x1 7.2 us: on_device(): pl.pallas_call(functools.partial(sweep_kernel, devices, groups, scale), o...]
    gather x2 -> x0, local copies, waits for them, and re-layouts: 2.83 us -> none  [the longest x1 2.08 us: on_device(): jnp.take(radiosity, jnp.maximum(asked - 1, 0), axis=0)]
    mul x2 -> x0, other arithmetic: 2.18 us -> none  [the longest x1 1.31 us: on_device(): ambient * old_root]
  transfers between devices with their start and end apart: 2 -> 0, of which waited for: 1 -> 0; matrix products, arithmetic and copies ran while one was open for 5% -> 0% of each run, Pallas kernels for 0% -> 0%
where the time goes in v1:
time: 37.8 us; the launch traced here: 37.5 us
  blocking collectives  26.6 us (70%)
  Pallas kernels  10.2 us (27%)
  between operations  0.63 us (2%)
    all_to_all x1, blocking collectives, on_device(): lax.all_to_all(packed, AXES, split_axis=0, concat_axis=0, tiled=True)  16.2 us
    all_to_all x1, blocking collectives, on_device(): lax.all_to_all(share, AXES, split_axis=0, concat_axis=0, tiled=True)  10.4 us
    pallas_call x1, Pallas kernels, on_device(): pl.pallas_call(functools.partial(sweep_kernel, devices, groups, scale), o...  7.2 us
    pallas_call x1, Pallas kernels, on_device(): pl.pallas_call(functools.partial(pack_kernel, devices, groups), out_shape...  1.61 us
    pallas_call x1, Pallas kernels, on_device(): pl.pallas_call(functools.partial(total_kernel, devices, groups, channels)...  1.4 us

profile of v1, /device:TPU:0, one launch (start us, length us, event | category | flops | bytes accessed | tf_op | source)
XLA Modules:
  0.0 37.5 jit_solution(6309964748329166779)
XLA Ops:
  0.6 1.6 %pack.1 = f32[416,1,128]{2,1,0:T(1,128)} custom-call(f32[3,4,128]{2,1,0:T(4,128)} %bitcast.6, f32[4,128]{1,0:T(4,128)} %area_ref.3, s32[4]{0:T(128)} %cluster_group_ref.3), custom_call_target="tpu_custom_call" | custom-call | tf_op jit(solution)/shard_map/pack/pallas_call | solution.py:182
  2.2 16.2 %all_to_all.10.gathered_ref = f32[416,1,128]{2,1,0:T(1,128)} all-to-all(f32[416,1,128]{2,1,0:T(1,128)} %pack.1), channel_id=1, replica_groups=mesh['grp'=4,'clu'=8] {'grp','clu'}, dimensions={0} | all-to-all | bytes 425984 | tf_op jit(solution)/shard_map/all_to_all | solution.py:189
  18.4 7.2 %sweep.1 = (f32[3,4,128]{2,1,0:T(4,128)}, f32[32,1,128]{2,1,0:T(1,128)}) custom-call(s32[128]{0:T(128)} %bitcast.10, s32[128]{0:T(128)} %source_slot_ref.1, s32[128]{0:T(128)} %receiver_slot_ref.1, s32[4]{0:T(128)} %cluster_group_ref.3, f32[3]{0:T(128)} %ambient_ref.1, f32[416,1,128]{2,1,0:T(1,128)} %all_to_all.10.gathered_ref, ...), custom_call_target="tpu_custom_call" | custom-call | tf_op jit(solution)/shard_map/sweep/pallas_call | solution.py:192
  25.6 10.4 %all_to_all.11.share_ref = f32[32,1,128]{2,1,0:T(1,128)} all-to-all(f32[32,1,128]{2,1,0:T(1,128)} %get-tuple-element.5), channel_id=1, replica_groups=mesh['grp'=4,'clu'=8] {'grp','clu'}, dimensions={0} | all-to-all | bytes 32768 | tf_op jit(solution)/shard_map/all_to_all | solution.py:215
  36.1 1.4 %total.1 = f32[3,16]{1,0:T(4,128)} custom-call(f32[32,1,128]{2,1,0:T(1,128)} %all_to_all.11.share_ref), custom_call_target="tpu_custom_call" | custom-call | tf_op jit(solution)/shard_map/total/pallas_call | solution.py:216

commit v2 on v1

--- a/solution.py
+++ b/solution.py
@@ -8,39 +8,86 @@
 from jax.sharding import PartitionSpec as P
 
 LANES = 128
+UNROLL = 4
 AXES = ("grp", "clu")
 VMEM = pl.BlockSpec(memory_space=pltpu.VMEM)
 SMEM = pl.BlockSpec(memory_space=pltpu.SMEM)
+HBM = pl.BlockSpec(memory_space=pltpu.HBM)
+DMA = pltpu.SemaphoreType.DMA
+
+
+def in_hbm(*arrays):
+    return tuple(pltpu.with_memory_space_constraint(a, pltpu.HBM) for a in arrays)
+
+
+def in_vmem(*arrays):
+    return tuple(pltpu.with_memory_space_constraint(a, pltpu.VMEM) for a in arrays)
 
 
 def rows_for(quantities, groups):
     return -(-quantities // (LANES // groups))
 
 
-def place(values, cluster_group_ref, groups):
+def start_all(pairs, sems):
+    copies = [pltpu.make_async_copy(src, dst, sems.at[i]) for i, (src, dst) in enumerate(pairs)]
+    for copy in copies:
+        copy.start()
+    return copies
+
+
+def pack_kernel(
+    devices,
+    groups,
+    radiosity_hbm,
+    area_hbm,
+    cluster_group_hbm,
+    source_device_hbm,
+    source_slot_hbm,
+    receiver_slot_hbm,
+    ambient_hbm,
+    out_ref,
+    cluster_group_ref,
+    source_device_ref,
+    source_slot_ref,
+    receiver_slot_ref,
+    ambient_ref,
+    radiosity_ref,
+    area_ref,
+    sems,
+):
+    channels, clusters, _ = radiosity_ref.shape
     per_row = LANES // groups
-    lane = lax.broadcasted_iota(jnp.int32, (1, LANES), 1)
-    rows = [jnp.zeros((1, LANES), jnp.float32) for _ in range(rows_for(len(values), groups))]
-    for q, of_clusters in enumerate(values):
-        for k, value in enumerate(of_clusters):
-            spot = (q % per_row) * groups + cluster_group_ref[k]
-            rows[q // per_row] += jnp.where(lane == spot, value, 0.0)
-    return rows
-
-
-def pack_kernel(devices, groups, radiosity_ref, area_ref, cluster_group_ref, out_ref):
-    channels, clusters, _ = radiosity_ref.shape
+    copies = start_all(
+        (
+            (radiosity_hbm, radiosity_ref),
+            (area_hbm, area_ref),
+            (cluster_group_hbm, cluster_group_ref),
+            (source_device_hbm, source_device_ref),
+            (source_slot_hbm, source_slot_ref),
+            (receiver_slot_hbm, receiver_slot_ref),
+            (ambient_hbm, ambient_ref),
+        ),
+        sems,
+    )
+    for copy in copies[:3]:
+        copy.wait()
     area = area_ref[...]
     sums = [
         jnp.sum(radiosity_ref[c] * area, axis=1, keepdims=True) for c in range(channels)
     ] + [jnp.sum(area, axis=1, keepdims=True)]
-    values = [[s[k : k + 1] for k in range(clusters)] for s in sums]
-    info = place(values, cluster_group_ref, groups)
+    lane = lax.broadcasted_iota(jnp.int32, (1, LANES), 1)
+    info = [jnp.zeros((1, LANES), jnp.float32) for _ in range(rows_for(channels + 1, groups))]
+    for q in range(channels + 1):
+        for k in range(clusters):
+            spot = (q % per_row) * groups + cluster_group_ref[k]
+            info[q // per_row] += jnp.where(lane == spot, sums[q][k : k + 1], 0.0)
     rows = [radiosity_ref[c, k : k + 1] for c in range(channels) for k in range(clusters)] + info
     block = len(rows)
     for d in range(devices):
         for r, row in enumerate(rows):
             out_ref[d * block + r] = row
+    for copy in copies[3:]:
+        copy.wait()
 
 
 def sweep_kernel(
@@ -116,7 +163,7 @@
                 acc_ref[k, c, b] += f * rows[c]
         return 0
 
-    lax.fori_loop(0, count, link, 0, unroll=4)
+    lax.fori_loop(0, count, link, 0, unroll=UNROLL)
 
     patch = lax.broadcasted_iota(jnp.int32, (blocks, 8, width), 0) * 8 + lax.broadcasted_iota(
         jnp.int32, (blocks, 8, width), 1
@@ -133,19 +180,26 @@
             )
             radiosity_ref[c, k : k + 1] = new
             sums[c][k] = jnp.sum(new * area_ref[k : k + 1], axis=1, keepdims=True)
-    rows = place(sums, cluster_group_ref, groups)
+    shares = [jnp.zeros((1, LANES), jnp.float32) for _ in range(rows_for(channels, groups))]
+    for c in range(channels):
+        for k in range(clusters):
+            spot = (c % per_row) * groups + cluster_group_ref[k]
+            shares[c // per_row] += jnp.where(lane == spot, sums[c][k], 0.0)
     wide_area = group_area
     for q in range(1, per_row):
         wide_area = jnp.where(lane >= q * groups, pltpu.roll(group_area, q * groups, 1), wide_area)
-    for r in range(len(rows)):
-        row = rows[r] / wide_area
+    for r in range(len(shares)):
+        row = shares[r] / wide_area
         for d in range(devices):
-            share_ref[d * len(rows) + r] = row
-
-
-def total_kernel(devices, groups, channels, share_ref, out_ref):
+            share_ref[d * len(shares) + r] = row
+
+
+def total_kernel(devices, groups, share_ref, new_ref, new_hbm, total_hbm, total_ref, sems):
+    channels = new_ref.shape[0]
     per_row = LANES // groups
     count = share_ref.shape[0] // devices
+    new_copy = pltpu.make_async_copy(new_ref, new_hbm, sems.at[0])
+    new_copy.start()
     rows = []
     for r in range(count):
         total = share_ref[r]
@@ -155,7 +209,11 @@
     for c in range(channels):
         row, shift = rows[c // per_row], (c % per_row) * groups
         part = pltpu.roll(row, LANES - shift, 1) if shift else row
-        out_ref[c : c + 1, :] = part[:, :groups]
+        total_ref[c : c + 1, :] = part[:, :groups]
+    total_copy = pltpu.make_async_copy(total_ref, total_hbm, sems.at[1])
+    total_copy.start()
+    new_copy.wait()
+    total_copy.wait()
 
 
 def on_device(
@@ -178,48 +236,79 @@
     scale = 2.0 * clusters / (width * count)
     block = channels * clusters + rows_for(channels + 1, groups)
     by_channel = functools.partial(jnp.transpose, axes=(1, 0, 2))
-
-    packed = pl.pallas_call(
+    f32, i32 = jnp.float32, jnp.int32
+    own = pltpu.VMEM((channels, clusters, width), f32)
+
+    packed, cluster_group, source_device, source_slot, receiver_slot, ambient = pl.pallas_call(
         functools.partial(pack_kernel, devices, groups),
-        out_shape=jax.ShapeDtypeStruct((devices * block, 1, LANES), jnp.float32),
-        in_specs=[VMEM, VMEM, SMEM],
-        out_specs=VMEM,
+        out_shape=(
+            pltpu.VMEM((devices * block, 1, LANES), f32),
+            pltpu.SMEM((clusters,), i32),
+            pltpu.SMEM((count,), i32),
+            pltpu.SMEM((count,), i32),
+            pltpu.SMEM((count,), i32),
+            pltpu.SMEM((channels,), f32),
+        ),
+        in_specs=[HBM] * 7,
+        out_specs=(VMEM,) + (SMEM,) * 5,
+        scratch_shapes=[
+            pltpu.VMEM((channels, clusters, width), f32),
+            pltpu.VMEM((clusters, width), f32),
+            DMA((7,)),
+        ],
+        compiler_params=pltpu.CompilerParams(vmem_limit_bytes=4 << 20),
+        cost_estimate=pl.CostEstimate(flops=10**10, transcendentals=0, bytes_accessed=10**8),
         name="pack",
-    )(by_channel(radiosity), patch_area, cluster_group)
+    )(
+        *in_hbm(
+            by_channel(radiosity),
+            patch_area,
+            cluster_group,
+            source_device[:, 0],
+            source_slot,
+            receiver_slot,
+            ambient,
+        )
+    )
     gathered = lax.all_to_all(packed, AXES, split_axis=0, concat_axis=0, tiled=True)
 
     share_rows = rows_for(channels, groups)
     new, share = pl.pallas_call(
         functools.partial(sweep_kernel, devices, groups, scale),
-        out_shape=(
-            jax.ShapeDtypeStruct((channels, clusters, width), jnp.float32),
-            jax.ShapeDtypeStruct((devices * share_rows, 1, LANES), jnp.float32),
-        ),
+        out_shape=(own, pltpu.VMEM((devices * share_rows, 1, LANES), f32)),
         in_specs=[SMEM] * 5 + [VMEM] * 6,
         out_specs=(VMEM, VMEM),
-        scratch_shapes=[pltpu.VMEM((clusters, channels, width // 8, 8, width), jnp.float32)],
+        scratch_shapes=[pltpu.VMEM((clusters, channels, width // 8, 8, width), f32)],
+        compiler_params=pltpu.CompilerParams(vmem_limit_bytes=16 << 20),
         name="sweep",
     )(
-        source_device[:, 0],
+        source_device,
         source_slot,
         receiver_slot,
         cluster_group,
         ambient,
-        gathered,
-        form_factors,
-        by_channel(emission),
-        by_channel(reflectance),
-        patch_area,
-        group_coupling,
+        *in_vmem(
+            gathered,
+            form_factors,
+            by_channel(emission),
+            by_channel(reflectance),
+            patch_area,
+            group_coupling,
+        ),
     )
     shares = lax.all_to_all(share, AXES, split_axis=0, concat_axis=0, tiled=True)
-    total = pl.pallas_call(
-        functools.partial(total_kernel, devices, groups, channels),
-        out_shape=jax.ShapeDtypeStruct((channels, groups), jnp.float32),
-        in_specs=[VMEM],
-        out_specs=VMEM,
+    new, total = pl.pallas_call(
+        functools.partial(total_kernel, devices, groups),
+        out_shape=(
+            pltpu.HBM((channels, clusters, width), f32),
+            pltpu.HBM((channels, groups), f32),
+        ),
+        in_specs=[VMEM, VMEM],
+        out_specs=(HBM, HBM),
+        scratch_shapes=[pltpu.VMEM((channels, groups), f32), DMA((2,))],
+        compiler_params=pltpu.CompilerParams(vmem_limit_bytes=4 << 20),
         name="total",
-    )(shares)
+    )(*in_vmem(shares, new))
     return by_channel(new), total.T
 
 

time: 37.8 us -> 31.9 us (0.84)
  Pallas kernels: 10.2 us -> 5.01 us
  blocking collectives: 26.6 us -> 26 us
    pallas_call x1, Pallas kernels: 7.2 us -> 3.26 us  [on_device(): pl.pallas_call(functools.partial(sweep_kernel, devices, groups, scale), o...]
    pallas_call x1, Pallas kernels: 1.4 us -> 0.68 us  [on_device(): pl.pallas_call(functools.partial(total_kernel, devices, groups), out_shap...]
    pallas_call x1, Pallas kernels: 1.61 us -> 1.07 us  [on_device(): pl.pallas_call(functools.partial(pack_kernel, devices, groups), out_shape...]
where the time goes in v2:
time: 31.9 us; the launch traced here: 31.7 us
  blocking collectives  26 us (82%)
  Pallas kernels  5.01 us (16%)
  between operations  0.71 us (2%)
    all_to_all x1, blocking collectives, on_device(): lax.all_to_all(packed, AXES, split_axis=0, concat_axis=0, tiled=True)  15.9 us
    all_to_all x1, blocking collectives, on_device(): lax.all_to_all(share, AXES, split_axis=0, concat_axis=0, tiled=True)  10.1 us
    pallas_call x1, Pallas kernels, on_device(): pl.pallas_call(functools.partial(sweep_kernel, devices, groups, scale), o...  3.26 us
    pallas_call x1, Pallas kernels, on_device(): pl.pallas_call(functools.partial(pack_kernel, devices, groups), out_shape...  1.07 us
    pallas_call x1, Pallas kernels, on_device(): pl.pallas_call(functools.partial(total_kernel, devices, groups), out_shap...  0.68 us

profile of v2, /device:TPU:0, one launch (start us, length us, event | category | flops | bytes accessed | tf_op | source)
XLA Modules:
  0.0 31.7 jit_solution(3399903514890552234)
XLA Ops:
  0.6 0.0 copy-start
  0.6 0.0 copy-start.1
  0.7 0.0 copy-start.2
  0.7 0.0 copy-start.3
  0.7 0.0 copy-start.4
  0.7 1.1 %pack.1 = (f32[416,1,128]{2,1,0:T(1,128)S(1)}, s32[4]{0:T(128)S(4)}, s32[128]{0:T(128)S(4)}, s32[128]{0:T(128)S(4)}, s32[128]{0:T(128)S(4)}, /*index=5*/f32[3]{0:T(128)S(4)}) custom-call(f32[3,4,128]{2,1,0:T(4,128)} %bitcast.8, f32[4,128]{1,0:T(4,128)} %area_ref.1, s32[4]{0:T(128)} %cluster_group_hbm.1, s32[128]{0:T(128)} %bitcast.11, s32[128]{0:T(128)} %source_slot_hbm.1, ...), custom_call_target="tpu_custom_call" | custom-call | flops 10000000000 | bytes 100000000 | tf_op jit(solution)/shard_map/pack/pallas_call | solution.py:242
  1.8 15.9 %all_to_all.10.gathered_ref = f32[416,1,128]{2,1,0:T(1,128)S(1)} all-to-all(f32[416,1,128]{2,1,0:T(1,128)S(1)} %get-tuple-element.17), channel_id=1, replica_groups=mesh['grp'=4,'clu'=8] {'grp','clu'}, dimensions={0} | all-to-all | bytes 425984 | tf_op jit(solution)/shard_map/all_to_all | solution.py:273
  17.6 0.0 copy-done
  17.6 0.0 copy-done.1
  17.6 0.0 copy-done.2
  17.6 0.0 copy-done.3
  17.6 0.0 copy-done.4
  17.7 3.3 %sweep.1 = (f32[3,4,128]{2,1,0:T(4,128)S(1)}, f32[32,1,128]{2,1,0:T(1,128)S(1)}) custom-call(s32[128]{0:T(128)S(4)} %get-tuple-element.12.source_device_ref, s32[128]{0:T(128)S(4)} %get-tuple-element.13.source_slot_ref, s32[128]{0:T(128)S(4)} %get-tuple-element.14.receiver_slot_ref, s32[4]{0:T(128)S(4)} %get-tuple-element.15.cluster_group_ref, ...), custom_call_target="tpu_custom_call" | custom-call | tf_op jit(solution)/shard_map/sweep/pallas_call | solution.py:276
  20.9 10.1 %all_to_all.11.share_ref = f32[32,1,128]{2,1,0:T(1,128)S(1)} all-to-all(f32[32,1,128]{2,1,0:T(1,128)S(1)} %get-tuple-element.18), channel_id=1, replica_groups=mesh['grp'=4,'clu'=8] {'grp','clu'}, dimensions={0} | all-to-all | bytes 32768 | tf_op jit(solution)/shard_map/all_to_all | solution.py:299
  31.1 0.7 %total.1 = (f32[3,4,128]{2,1,0:T(4,128)}, f32[3,16]{1,0:T(4,128)}) custom-call(f32[32,1,128]{2,1,0:T(1,128)S(1)} %all_to_all.11.share_ref, f32[3,4,128]{2,1,0:T(4,128)S(1)} %get-tuple-element.19.new_ref), custom_call_target="tpu_custom_call" | custom-call | tf_op jit(solution)/shard_map/total/pallas_call | solution.py:300
Async XLA Ops:
  0.6 17.0 %copy-start = (f32[128,128,128]{2,1,0:T(8,128)S(1)}, f32[128,128,128]{2,1,0:T(8,128)}, u32[]{:S(2)}) copy-start(f32[128,128,128]{2,1,0:T(8,128)} %factors_ref.1) | copy-start | bytes 25165828
  0.6 17.0 %copy-start.1 = (f32[16,16]{1,0:T(8,128)S(1)}, f32[16,16]{1,0:T(8,128)}, u32[]{:S(2)}) copy-start(f32[16,16]{1,0:T(8,128)} %coupling_ref.1) | copy-start | bytes 3076
  0.7 17.0 %copy-start.2 = (f32[4,3,128]{2,0,1:T(4,128)S(1)}, f32[4,3,128]{2,0,1:T(4,128)}, u32[]{:S(2)}) copy-start(f32[4,3,128]{2,0,1:T(4,128)} %param.16) | copy-start | bytes 18436
  0.7 17.0 %copy-start.3 = (f32[4,3,128]{2,0,1:T(4,128)S(1)}, f32[4,3,128]{2,0,1:T(4,128)}, u32[]{:S(2)}) copy-start(f32[4,3,128]{2,0,1:T(4,128)} %param.17) | copy-start | bytes 18436
  0.7 17.0 %copy-start.4 = (f32[4,128]{1,0:T(4,128)S(1)}, f32[4,128]{1,0:T(4,128)}, u32[]{:S(2)}) copy-start(f32[4,128]{1,0:T(4,128)} %area_ref.1) | copy-start | bytes 6148

commit v3 on v2

--- a/solution.py
+++ b/solution.py
@@ -9,6 +9,7 @@
 
 LANES = 128
 UNROLL = 4
+STEP = 8
 AXES = ("grp", "clu")
 VMEM = pl.BlockSpec(memory_space=pltpu.VMEM)
 SMEM = pl.BlockSpec(memory_space=pltpu.SMEM)
@@ -37,6 +38,7 @@
 
 def pack_kernel(
     devices,
+    pair_stride,
     groups,
     radiosity_hbm,
     area_hbm,
@@ -81,48 +83,65 @@
         for k in range(clusters):
             spot = (q % per_row) * groups + cluster_group_ref[k]
             info[q // per_row] += jnp.where(lane == spot, sums[q][k : k + 1], 0.0)
-    rows = [radiosity_ref[c, k : k + 1] for c in range(channels) for k in range(clusters)] + info
-    block = len(rows)
+    half = clusters // 2
+    halves = [
+        [(0, k) for k in range(clusters)] + [(1, k) for k in range(half)],
+        [(2, k) for k in range(clusters)] + [(1, k) for k in range(half, clusters)],
+    ]
+    block = len(halves[0]) + len(info)
     for d in range(devices):
+        rows = [radiosity_ref[c, k : k + 1] for c, k in halves[d // pair_stride % 2]] + info
         for r, row in enumerate(rows):
             out_ref[d * block + r] = row
     for copy in copies[3:]:
         copy.wait()
 
 
-def sweep_kernel(
+def column_sums(acc, diagonal):
+    column = jnp.sum(acc, axis=2, keepdims=True)
+    spread = jnp.sum(jnp.where(diagonal, column, 0.0), axis=0)
+    return jnp.sum(spread, axis=0, keepdims=True)
+
+
+def diagonal_mask(width):
+    shape = (width // 8, 8, width)
+    patch = lax.broadcasted_iota(jnp.int32, shape, 0) * 8 + lax.broadcasted_iota(jnp.int32, shape, 1)
+    return patch == lax.broadcasted_iota(jnp.int32, shape, 2)
+
+
+def first_kernel(
     devices,
     groups,
-    scale,
     source_device_ref,
     source_slot_ref,
     receiver_slot_ref,
     cluster_group_ref,
     ambient_ref,
-    gathered_ref,
+    own_ref,
     factors_ref,
-    emission_ref,
-    reflectance_ref,
-    area_ref,
     coupling_ref,
-    radiosity_ref,
-    share_ref,
+    plan_ref,
+    rows_ref,
     acc_ref,
 ):
-    channels, clusters, width = emission_ref.shape
-    count = factors_ref.shape[0]
-    blocks = width // 8
-    block_rows = gathered_ref.shape[0] // devices
-    own_rows = channels * clusters
+    count, width, _ = factors_ref.shape
+    clusters, blocks = acc_ref.shape[:2]
+    channels = ambient_ref.shape[0]
+    capacity = count + STEP
+    table = clusters * capacity
+    half = clusters // 2
+    block_rows = own_ref.shape[0] // devices
+    own_rows = clusters + half
     per_row = LANES // groups
+    core = lax.rem(lax.axis_index("grp"), 2)
 
     acc_ref[...] = jnp.zeros_like(acc_ref)
 
     totals = []
     for r in range(own_rows, block_rows):
-        total = gathered_ref[r]
+        total = own_ref[r]
         for d in range(1, devices):
-            total = total + gathered_ref[d * block_rows + r]
+            total = total + own_ref[d * block_rows + r]
         totals.append(total)
     lane = lax.broadcasted_iota(jnp.int32, (1, LANES), 1)
     inside = lane < groups
@@ -133,63 +152,128 @@
         parts.append(jnp.where(inside, part, 0.0))
     group_area = jnp.where(inside, parts[channels], 1.0)
     all_area = jnp.sum(parts[channels], axis=1, keepdims=True)
-    coarse = []
     for c in range(channels):
         old_group = parts[c] / group_area
         root = ambient_ref[c] * (jnp.sum(parts[c], axis=1, keepdims=True) / all_area)
-        coarse.append(
-            [
-                jnp.sum(
-                    coupling_ref[pl.ds(cluster_group_ref[k], 1), :] * old_group[:, :groups],
-                    axis=1,
-                    keepdims=True,
-                )
-                / groups
-                + root
-                for k in range(clusters)
-            ]
-        )
-
-    def link(l, _):
-        first = source_device_ref[l] * block_rows + source_slot_ref[l]
-        k = receiver_slot_ref[l]
-        rows = [
-            jnp.broadcast_to(gathered_ref[first + c * clusters], (8, width))
-            for c in range(channels)
-        ]
-        for b in range(blocks):
-            f = factors_ref[l, b * 8 : (b + 1) * 8, :]
-            for c in range(channels):
-                acc_ref[k, c, b] += f * rows[c]
-        return 0
-
-    lax.fori_loop(0, count, link, 0, unroll=UNROLL)
-
-    patch = lax.broadcasted_iota(jnp.int32, (blocks, 8, width), 0) * 8 + lax.broadcasted_iota(
-        jnp.int32, (blocks, 8, width), 1
-    )
-    diagonal = patch == lax.broadcasted_iota(jnp.int32, (blocks, 8, width), 2)
-    sums = [[None] * clusters for _ in range(channels)]
-    for k in range(clusters):
-        for c in range(channels):
-            column = jnp.sum(acc_ref[k, c], axis=2, keepdims=True)
-            spread = jnp.sum(jnp.where(diagonal, column, 0.0), axis=0)
-            irradiance = jnp.sum(spread, axis=0, keepdims=True) * scale
-            new = emission_ref[c, k : k + 1] + reflectance_ref[c, k : k + 1] * (
-                irradiance + coarse[c][k]
+        for k in range(clusters):
+            coupling = coupling_ref[pl.ds(cluster_group_ref[k], 1), :]
+            coarse = (
+                jnp.sum(coupling * old_group[:, :groups], axis=1, keepdims=True) / groups + root
             )
-            radiosity_ref[c, k : k + 1] = new
-            sums[c][k] = jnp.sum(new * area_ref[k : k + 1], axis=1, keepdims=True)
-    shares = [jnp.zeros((1, LANES), jnp.float32) for _ in range(rows_for(channels, groups))]
-    for c in range(channels):
-        for k in range(clusters):
-            spot = (c % per_row) * groups + cluster_group_ref[k]
-            shares[c // per_row] += jnp.where(lane == spot, sums[c][k], 0.0)
+            rows_ref[clusters + c * clusters + k] = jnp.broadcast_to(coarse, (1, LANES))
     wide_area = group_area
     for q in range(1, per_row):
         wide_area = jnp.where(lane >= q * groups, pltpu.roll(group_area, q * groups, 1), wide_area)
+    rows_ref[clusters + channels * clusters] = wide_area
+
+    def link(l, filled):
+        k = receiver_slot_ref[l]
+        slot = source_slot_ref[l]
+        base = source_device_ref[l] * block_rows
+        spot = k * capacity + (lax.shift_right_arithmetic(filled, k * 8) & 255)
+        upper = (slot >= half).astype(jnp.int32)
+        mine = (upper == core).astype(jnp.int32)
+        plan_ref[spot] = l
+        plan_ref[table + spot] = base + slot
+        plan_ref[2 * table + spot] = (base + clusters + slot - upper * half) * 2 + mine
+        row = jnp.broadcast_to(own_ref[base + slot], (8, width))
+        for b in range(blocks):
+            acc_ref[k, b] += factors_ref[l, b * 8 : (b + 1) * 8, :] * row
+        return filled + lax.shift_left(jnp.int32(1), k * 8)
+
+    filled = lax.fori_loop(0, count, link, jnp.int32(0), unroll=UNROLL)
+    for k in range(clusters):
+        length = lax.shift_right_arithmetic(filled, jnp.int32(k * 8)) & 255
+        plan_ref[3 * table + k] = length
+        for i in range(STEP - 1):
+            for part in range(3):
+                plan_ref[part * table + k * capacity + length + i] = 0
+
+    diagonal = diagonal_mask(width)
+    for k in range(clusters):
+        rows_ref[k] = column_sums(acc_ref[k], diagonal)
+
+
+def second_kernel(
+    devices,
+    groups,
+    scale,
+    plan_ref,
+    cluster_group_ref,
+    own_ref,
+    other_ref,
+    factors_ref,
+    rows_ref,
+    emission_ref,
+    reflectance_ref,
+    area_ref,
+    radiosity_ref,
+    share_ref,
+    acc_ref,
+):
+    channels, clusters, width = emission_ref.shape
+    count = factors_ref.shape[0]
+    capacity = count + STEP
+    table = clusters * capacity
+    blocks = width // 8
+    per_row = LANES // groups
+    core = lax.rem(lax.axis_index("grp"), 2)
+
+    acc_ref[...] = jnp.zeros_like(acc_ref)
+    for k in range(clusters):
+        length = plan_ref[3 * table + k]
+
+        def step(j, _, k=k, length=length):
+            links, pairs = [], []
+            for u in range(STEP):
+                spot = k * capacity + j * STEP + u
+                links.append(plan_ref[spot])
+                outer = other_ref[plan_ref[table + spot]]
+                code = plan_ref[2 * table + spot]
+                middle = lax.shift_right_logical(code, jnp.int32(1))
+                inner = jnp.where((code & 1) == 1, own_ref[middle], other_ref[middle])
+                valid = j * STEP + u < length
+                pairs.append(
+                    [
+                        jnp.broadcast_to(jnp.where(valid, row, 0.0), (8, width))
+                        for row in (inner, outer)
+                    ]
+                )
+            for b in range(blocks):
+                acc = [acc_ref[k, r, b] for r in range(2)]
+                for u in range(STEP):
+                    f = factors_ref[links[u], b * 8 : (b + 1) * 8, :]
+                    for r in range(2):
+                        acc[r] += f * pairs[u][r]
+                for r in range(2):
+                    acc_ref[k, r, b] = acc[r]
+            return 0
+
+        lax.fori_loop(0, lax.div(length + STEP - 1, STEP), step, 0)
+
+    diagonal = diagonal_mask(width)
+    lane = lax.broadcasted_iota(jnp.int32, (1, LANES), 1)
+    shares = [jnp.zeros((1, LANES), jnp.float32) for _ in range(rows_for(channels, groups))]
+    for k in range(clusters):
+        mine = rows_ref[k]
+        middle = column_sums(acc_ref[k, 0], diagonal)
+        others = column_sums(acc_ref[k, 1], diagonal)
+        by_channel = (
+            jnp.where(core == 0, mine, others),
+            middle,
+            jnp.where(core == 0, others, mine),
+        )
+        for c in range(channels):
+            coarse = rows_ref[clusters + c * clusters + k]
+            new = emission_ref[c, k : k + 1] + reflectance_ref[c, k : k + 1] * (
+                by_channel[c] * scale + coarse
+            )
+            radiosity_ref[c, k : k + 1] = new
+            pulled = jnp.sum(new * area_ref[k : k + 1], axis=1, keepdims=True)
+            spot = (c % per_row) * groups + cluster_group_ref[k]
+            shares[c // per_row] += jnp.where(lane == spot, pulled, 0.0)
     for r in range(len(shares)):
-        row = shares[r] / wide_area
+        row = shares[r] / rows_ref[clusters + channels * clusters]
         for d in range(devices):
             share_ref[d * len(shares) + r] = row
 
@@ -234,13 +318,15 @@
     groups = group_coupling.shape[0]
     devices = lax.axis_size("grp") * lax.axis_size("clu")
     scale = 2.0 * clusters / (width * count)
-    block = channels * clusters + rows_for(channels + 1, groups)
+    pair_stride = lax.axis_size("clu")
+    block = clusters + clusters // 2 + rows_for(channels + 1, groups)
+    plan_size = 3 * clusters * (count + STEP) + clusters
     by_channel = functools.partial(jnp.transpose, axes=(1, 0, 2))
     f32, i32 = jnp.float32, jnp.int32
     own = pltpu.VMEM((channels, clusters, width), f32)
 
     packed, cluster_group, source_device, source_slot, receiver_slot, ambient = pl.pallas_call(
-        functools.partial(pack_kernel, devices, groups),
+        functools.partial(pack_kernel, devices, pair_stride, groups),
         out_shape=(
             pltpu.VMEM((devices * block, 1, LANES), f32),
             pltpu.SMEM((clusters,), i32),
@@ -270,30 +356,51 @@
             ambient,
         )
     )
-    gathered = lax.all_to_all(packed, AXES, split_axis=0, concat_axis=0, tiled=True)
-
-    share_rows = rows_for(channels, groups)
-    new, share = pl.pallas_call(
-        functools.partial(sweep_kernel, devices, groups, scale),
-        out_shape=(own, pltpu.VMEM((devices * share_rows, 1, LANES), f32)),
-        in_specs=[SMEM] * 5 + [VMEM] * 6,
-        out_specs=(VMEM, VMEM),
-        scratch_shapes=[pltpu.VMEM((clusters, channels, width // 8, 8, width), f32)],
+    own_half = lax.all_to_all(packed, AXES, split_axis=0, concat_axis=0, tiled=True)
+    other_half = lax.ppermute(
+        own_half, "grp", [(i, i ^ 1) for i in range(lax.axis_size("grp"))]
+    )
+
+    plan, rows = pl.pallas_call(
+        functools.partial(first_kernel, devices, groups),
+        out_shape=(
+            pltpu.SMEM((plan_size,), i32),
+            pltpu.VMEM((clusters + channels * clusters + 1, 1, LANES), f32),
+        ),
+        in_specs=[SMEM] * 5 + [VMEM] * 3,
+        out_specs=(SMEM, VMEM),
+        scratch_shapes=[pltpu.VMEM((clusters, width // 8, 8, width), f32)],
         compiler_params=pltpu.CompilerParams(vmem_limit_bytes=16 << 20),
-        name="sweep",
+        cost_estimate=pl.CostEstimate(flops=10**8, transcendentals=0, bytes_accessed=10**7),
+        name="first",
     )(
         source_device,
         source_slot,
         receiver_slot,
         cluster_group,
         ambient,
+        *in_vmem(own_half, form_factors, group_coupling),
+    )
+    share_rows = rows_for(channels, groups)
+    new, share = pl.pallas_call(
+        functools.partial(second_kernel, devices, groups, scale),
+        out_shape=(own, pltpu.VMEM((devices * share_rows, 1, LANES), f32)),
+        in_specs=[SMEM] * 2 + [VMEM] * 7,
+        out_specs=(VMEM, VMEM),
+        scratch_shapes=[pltpu.VMEM((clusters, 2, width // 8, 8, width), f32)],
+        compiler_params=pltpu.CompilerParams(vmem_limit_bytes=16 << 20),
+        name="second",
+    )(
+        plan,
+        cluster_group,
         *in_vmem(
-            gathered,
+            own_half,
+            other_half,
             form_factors,
+            rows,
             by_channel(emission),
             by_channel(reflectance),
             patch_area,
-            group_coupling,
         ),
     )
     shares = lax.all_to_all(share, AXES, split_axis=0, concat_axis=0, tiled=True)

time: 31.9 us -> 30.8 us (0.966)
  blocking collectives: 26 us -> 23.8 us
  Pallas kernels: 5.01 us -> 5.98 us
    all_to_all x1, blocking collectives: 10.1 us -> 8.94 us  [on_device(): lax.all_to_all(share, AXES, split_axis=0, concat_axis=0, tiled=True)]
    all_to_all x1, blocking collectives: 15.9 us -> 14.8 us  [on_device(): lax.all_to_all(packed, AXES, split_axis=0, concat_axis=0, tiled=True)]
    pallas_call x2 -> x3, Pallas kernels: 4.33 us -> 5.3 us  [the longest x1 2.42 us: on_device(): pl.pallas_call(functools.partial(second_kernel, devices, groups, scale),...]
  transfers between devices with their start and end apart: 0 -> 1, of which waited for: 0 -> 0; matrix products, arithmetic and copies ran while one was open for 0% -> 0% of each run, Pallas kernels for 0% -> 6%
where the time goes in v3:
time: 30.8 us; the launch traced here: 30.6 us
  blocking collectives  23.8 us (77%)
  Pallas kernels  5.98 us (19%)
  between operations  0.72 us (2%)
    all_to_all x1, blocking collectives, on_device(): lax.all_to_all(packed, AXES, split_axis=0, concat_axis=0, tiled=True)  14.8 us
    all_to_all x1, blocking collectives, on_device(): lax.all_to_all(share, AXES, split_axis=0, concat_axis=0, tiled=True)  8.94 us
    pallas_call x1, Pallas kernels, on_device(): pl.pallas_call(functools.partial(second_kernel, devices, groups, scale),...  2.42 us
    pallas_call x1, Pallas kernels, on_device(): pl.pallas_call(functools.partial(first_kernel, devices, groups), out_shap...  1.82 us
    pallas_call x1, Pallas kernels, on_device(): pl.pallas_call(functools.partial(pack_kernel, devices, pair_stride, group...  1.06 us
    pallas_call x1, Pallas kernels, on_device(): pl.pallas_call(functools.partial(total_kernel, devices, groups), out_shap...  0.68 us
  transfers between devices with their start and end apart: 1, of which 0 were waited for; matrix products, arithmetic and copies ran while one was open for 0% of the time, Pallas kernels for 6%

profile of v3, /device:TPU:0, one launch (start us, length us, event | category | flops | bytes accessed | tf_op | source)
XLA Modules:
  0.0 30.6 jit_solution(10633180165374167062)
XLA Ops:
  0.6 0.0 copy-start
  0.6 0.0 copy-start.1
  0.7 1.1 %pack.1 = (f32[224,1,128]{2,1,0:T(1,128)S(1)}, s32[4]{0:T(128)S(4)}, s32[128]{0:T(128)S(4)}, s32[128]{0:T(128)S(4)}, s32[128]{0:T(128)S(4)}, /*index=5*/f32[3]{0:T(128)S(4)}) custom-call(f32[3,4,128]{2,1,0:T(4,128)} %bitcast.8, f32[4,128]{1,0:T(4,128)} %area_ref.1, s32[4]{0:T(128)} %cluster_group_hbm.1, s32[128]{0:T(128)} %bitcast.11, s32[128]{0:T(128)} %source_slot_hbm.1, ...), custom_call_target="tpu_custom_call" | custom-call | flops 10000000000 | bytes 100000000 | tf_op jit(solution)/shard_map/pack/pallas_call | solution.py:328
  1.7 0.0 copy-start.2
  1.7 0.0 copy-start.3
  1.7 0.0 copy-start.4
  1.8 14.8 %all_to_all.10.own_ref = f32[224,1,128]{2,1,0:T(1,128)S(1)} all-to-all(f32[224,1,128]{2,1,0:T(1,128)S(1)} %get-tuple-element.19), channel_id=1, replica_groups=mesh['grp'=4,'clu'=8] {'grp','clu'}, dimensions={0} | all-to-all | bytes 229376 | tf_op jit(solution)/shard_map/all_to_all | solution.py:359
  16.6 0.1 collective-permute-start
  16.7 0.0 copy-done
  16.7 0.0 copy-done.1
  16.7 1.8 %first.1 = (s32[1636]{0:T(1024)S(4)}, f32[17,1,128]{2,1,0:T(1,128)S(1)}) custom-call(s32[128]{0:T(128)S(4)} %get-tuple-element.14.source_device_ref, s32[128]{0:T(128)S(4)} %get-tuple-element.15.source_slot_ref, s32[128]{0:T(128)S(4)} %get-tuple-element.16.receiver_slot_ref, s32[4]{0:T(128)S(4)} %get-tuple-element.17.cluster_group_ref, ...), custom_call_target="tpu_custom_call" | custom-call | flops 100000000 | bytes 10000000 | tf_op jit(solution)/shard_map/first/pallas_call | solution.py:364
  18.6 0.0 collective-permute-done.other_ref
  18.6 0.0 copy-done.2
  18.6 0.0 copy-done.3
  18.6 0.0 copy-done.4
  18.6 2.4 %second.1 = (f32[3,4,128]{2,1,0:T(4,128)S(1)}, f32[32,1,128]{2,1,0:T(1,128)S(1)}) custom-call(s32[1636]{0:T(1024)S(4)} %get-tuple-element.20.plan_ref, s32[4]{0:T(128)S(4)} %get-tuple-element.17.cluster_group_ref, f32[224,1,128]{2,1,0:T(1,128)S(1)} %all_to_all.10.own_ref, f32[224,1,128]{2,1,0:T(1,128)S(1)} %collective-permute-done.other_ref, ...), custom_call_target="tpu_custom_call" | custom-call | tf_op jit(solution)/shard_map/second/pallas_call | solution.py:385
  21.0 8.9 %all_to_all.11.share_ref = f32[32,1,128]{2,1,0:T(1,128)S(1)} all-to-all(f32[32,1,128]{2,1,0:T(1,128)S(1)} %get-tuple-element.22), channel_id=1, replica_groups=mesh['grp'=4,'clu'=8] {'grp','clu'}, dimensions={0} | all-to-all | bytes 32768 | tf_op jit(solution)/shard_map/all_to_all | solution.py:406
  30.0 0.7 %total.1 = (f32[3,4,128]{2,1,0:T(4,128)}, f32[3,16]{1,0:T(4,128)}) custom-call(f32[32,1,128]{2,1,0:T(1,128)S(1)} %all_to_all.11.share_ref, f32[3,4,128]{2,1,0:T(4,128)S(1)} %get-tuple-element.23.new_ref), custom_call_target="tpu_custom_call" | custom-call | tf_op jit(solution)/shard_map/total/pallas_call | solution.py:407
Async XLA Ops:
  0.6 16.1 %copy-start = (f32[128,128,128]{2,1,0:T(8,128)S(1)}, f32[128,128,128]{2,1,0:T(8,128)}, u32[]{:S(2)}) copy-start(f32[128,128,128]{2,1,0:T(8,128)} %factors_ref.3) | copy-start | bytes 25165828
  0.6 16.1 %copy-start.1 = (f32[16,16]{1,0:T(8,128)S(1)}, f32[16,16]{1,0:T(8,128)}, u32[]{:S(2)}) copy-start(f32[16,16]{1,0:T(8,128)} %coupling_ref.1) | copy-start | bytes 3076
  1.7 16.8 %copy-start.2 = (f32[4,3,128]{2,0,1:T(4,128)S(1)}, f32[4,3,128]{2,0,1:T(4,128)}, u32[]{:S(2)}) copy-start(f32[4,3,128]{2,0,1:T(4,128)} %param.16) | copy-start | bytes 18436
  1.7 16.8 %copy-start.3 = (f32[4,3,128]{2,0,1:T(4,128)S(1)}, f32[4,3,128]{2,0,1:T(4,128)}, u32[]{:S(2)}) copy-start(f32[4,3,128]{2,0,1:T(4,128)} %param.17) | copy-start | bytes 18436
  1.7 16.8 %copy-start.4 = (f32[4,128]{1,0:T(4,128)S(1)}, f32[4,128]{1,0:T(4,128)}, u32[]{:S(2)}) copy-start(f32[4,128]{1,0:T(4,128)} %area_ref.1) | copy-start | bytes 6148
  16.6 2.0 %collective-permute-start = (f32[224,1,128]{2,1,0:T(1,128)S(1)}, f32[224,1,128]{2,1,0:T(1,128)S(1)}, u32[]{:S(2)}, u32[]{:S(2)}) collective-permute-start(f32[224,1,128]{2,1,0:T(1,128)S(1)} %all_to_all.10.own_ref), channel_id=1, source_target_pairs={{0,8},{8,0},{16,24},{24,16},{1,9},{9,1},{17,25},{25,17},{2,10},{10... | collective-permute-start | bytes 344072 | tf_op jit(solution)/shard_map/ppermute | solution.py:360
